TPU v7x, 512 devices: a whole 4x8x8 slice. The times are simulated.
512 devices in a mesh: section: 4 (over y_lo), row: 16 (over z, core), col: 8 (over y_hi, x).
Axes of the slice: x: 4, y: 8 (y_hi: 2, y_lo: 4; y = y_hi * 4 + y_lo), z: 8, core: 2. Of those that a mesh axis runs over, the one named last changes fastest.
Arguments:
- section_input: bfloat16 [4, 2, 128, 128, 128], P('section', None, 'row', 'col'), may hold values from -6 to 6
- first_pre: bfloat16 [4, 2, 128, 128, 128], P('section', None, 'row', 'col'), may hold values from -6 to 6
- second_pre: bfloat16 [4, 2, 128, 128, 128], P('section', None, 'row', 'col'), may hold values from -6 to 6
- out_grad: bfloat16 [2, 128, 128, 128], P(None, 'row', 'col'), may hold values from -6 to 6
- kernels: bfloat16 [4, 2, 3, 3, 128, 128], P('section'), may hold values from -0.1875 to 0.1875
- bn_scale: float32 [4, 2, 128], P('section'), may hold values from 0.5 to 2
- bn_shift: float32 [4, 2, 128], P('section'), may hold values from -3 to 3
Outputs:
- input_grad: bfloat16 [4, 2, 128, 128, 128], P('section', None, 'row', 'col')
- filter_grad: float32 [4, 2, 3, 3, 128, 128], P('section')
All inputs are finite; a program needn't handle non-finite values.
Results may differ from a plain program's by a relative error of at most 0.013.
Values may be sent and summed in bfloat16 or wider, within the bound.
No kernel may reach another device: no remote copies, remote signals or barrier semaphores. Data moves between devices by JAX's collectives and lax.ppermute only.
A program may use at most 64 MiB of HBM per device.

v0:
```python
import functools

import jax
import jax.numpy as jnp
from jax import lax
from jax.experimental import pallas as pl
from jax.experimental.pallas import tpu as pltpu
from jax.sharding import Mesh
from jax.sharding import PartitionSpec as P

ROW = ("row_0", "row_1")
COL = ("col_0", "col_1")
NEAR = ("row_1", "col_1")
FAR = ("row_0", "col_0")
VMEM = pl.BlockSpec(memory_space=pltpu.VMEM)
SMEM = pl.BlockSpec(memory_space=pltpu.SMEM)
PARAMS = pltpu.CompilerParams(vmem_limit_bytes=24 * 1024 * 1024)


DEPTH = 8
NARROW = 4
PACKED = 2


def prepare_kernel(flags, *refs):
    sources = refs[:6]
    masks, inward, outward, act, kept, fields, norms, done = refs[6:]
    targets = [fields.at[k] for k in range(4)] + [norms.at[k] for k in range(2)]
    moves = [
        pltpu.make_async_copy(source, target, done.at[k])
        for k, (source, target) in enumerate(zip(sources, targets))
    ]
    for move in moves:
        move.start()
    for move in moves:
        move.wait()
    inputs, first_pre, second_pre, out_grad = [fields[k].astype(jnp.float32) for k in range(4)]
    scale, shift = (norms[0], norms[1])
    kept[...] = scale
    width = masks.shape[3]
    first_norm = scale[0] * first_pre + shift[0]
    act[...] = jnp.maximum(first_norm, 0.0).astype(jnp.bfloat16)
    alive = scale[1] * second_pre + shift[1] + inputs > 0
    passing = jnp.where(flags[0] > 0, out_grad, 1.0)
    passed = jnp.where(alive, passing, 0.0)
    on = jnp.where(first_norm > 0, 1.0, 0.0)
    for kind, value in enumerate((passed, on)):
        masks[kind] = value.astype(jnp.bfloat16)
        head = value[:, :, :DEPTH]
        tail = value[:, :, width - DEPTH :]
        inward[kind] = jnp.where(flags[1] > 0, tail, head).astype(jnp.bfloat16)
        outward[kind] = jnp.where(flags[1] > 0, head, tail).astype(jnp.bfloat16)


def correlate(field, kernel):
    rows, cols, width = field.shape
    rows -= 2
    slabs = [field[i : i + rows].reshape(rows * cols, width) for i in range(3)]
    parts = jnp.dot(jnp.concatenate(slabs, axis=1), kernel[...], preferred_element_type=jnp.float32)
    before, here, after = [parts[:, j * width : (j + 1) * width] for j in range(3)]
    total = pltpu.roll(before, 1, 0) + here + pltpu.roll(after, rows * cols - 1, 0)
    return total.reshape(rows, cols, width)


def unit(masks, micro, incoming, first, second, scale, reach):
    top = DEPTH - reach - 2
    rows = masks.shape[2] - 2 * top
    masked = masks[0, micro, top : top + rows].astype(jnp.float32)
    if incoming is not None:
        masked = masked * incoming
    second_grad = (scale[1] * masked).astype(jnp.bfloat16)
    on = masks[1, micro, top + 1 : top + rows - 1].astype(jnp.float32)
    first_grad = (scale[0] * (correlate(second_grad, second) * on)).astype(jnp.bfloat16)
    result = masked[2 : rows - 2] + correlate(first_grad, first)
    return (result, first_grad, second_grad)


def packed(cells, pairs, pack, cut):
    rows, cols, width = cells.shape
    half = rows // 2
    kept = cols - 2 * cut
    pairs[:half] = cells.reshape(half, 2, cols, width)
    for k in range(2):
        pack[:half, k * kept : (k + 1) * kept] = pairs[:half, k, cut : cut + kept]
    return pack[:half]


def unpacked(cells, pairs, pack, skip):
    half = cells.shape[0] - skip
    kept = cells.shape[1] // 2
    cols = pairs.shape[2]
    cut = (cols - kept) // 2
    pack[:half] = cells[skip // 2 : skip // 2 + half].astype(jnp.float32)
    pairs[:half] = jnp.zeros((half, *pairs.shape[1:]), jnp.float32)
    for k in range(2):
        pairs[:half, k, cut : cut + kept] = pack[:half, k * kept : (k + 1) * kept]
    return pairs[:half].reshape(2 * half, cols, pairs.shape[3])


def widened(cells, frame, skip):
    rows = cells.shape[0] - 2 * skip
    value = cells[skip : skip + rows].astype(jnp.float32)
    frame[:rows] = jnp.zeros((rows, *frame.shape[1:]), jnp.float32)
    frame[:rows, NARROW : frame.shape[1] - NARROW] = value
    return frame[:rows]


def stage_kernel(*refs, micro, step, reach):
    active, masks, first, second, scale, *received, out, frame, pairs, pack = refs

    @pl.when(active[0] > 0)
    def _():
        incoming = None
        if step == 1:
            incoming = unpacked(received[0], pairs, pack, 0)
        elif step > 1:
            incoming = widened(received[0], frame, 0)
        result, _, _ = unit(masks, micro, incoming, first, second, scale, reach)
        if step:
            frame[: result.shape[0]] = result
            result = frame[: result.shape[0], NARROW : result.shape[1] - NARROW]
        else:
            result = packed(result, pairs, pack, PACKED)
        out[...] = result.astype(jnp.bfloat16)


def filter_grad(cells, field):
    rows, cols, width = field.shape
    flat = field.astype(jnp.float32).reshape(rows * cols, width)
    turned = (pltpu.roll(flat, rows * cols - 1, 0), flat, pltpu.roll(flat, 1, 0))
    spread = [
        t.reshape(rows, cols, width)[:, DEPTH : cols - DEPTH].astype(jnp.bfloat16) for t in turned
    ]
    height = cells.shape[0]
    sides = [
        spread[j][2 - i : 2 - i + height].reshape(-1, width) for i in range(3) for j in range(3)
    ]
    return lax.dot_general(
        cells.reshape(-1, width),
        jnp.concatenate(sides, axis=1),
        (((0,), (0,)), ((), ())),
        preferred_element_type=jnp.float32,
    )


def settle(last, masks, micro, received, first, second, scale, frame, pairs, pack):
    incoming = jnp.where(last[0] > 0, 1.0, 0.0)
    steps = len(received)
    for step, cells in enumerate(received):
        skip = 2 * (steps - 1 - step)
        if step:
            incoming = incoming + widened(cells, frame.at[step], skip)
        else:
            incoming = incoming + unpacked(cells, pairs, pack, skip)
    result, first_grad, second_grad = unit(masks, micro, incoming, first, second, scale, 0)
    tile = result[:, DEPTH : result.shape[1] - DEPTH].astype(jnp.bfloat16)
    return (tile, first_grad, second_grad[1:-1])


def early_kernel(*refs, micro):
    last, masks, first, second, scale, inputs, act, *received = refs
    tile, sums, frame, pairs, pack = received[-5:]
    received = received[:-5]
    values = settle(last, masks, micro, received, first, second, scale, frame, pairs, pack)
    tile[...] = values[0]
    for which, cells in enumerate((inputs, act)):
        sums[which] = filter_grad(cells[micro], values[1 + which])


def last_kernel(*refs, micros, early):
    last, masks, first, second, scale, inputs, act, *rest = refs
    out, partial, frame, pairs, pack = rest[-5:]
    ready = rest[: 2 * early]
    received = rest[2 * early : -5]
    micro = micros - 1
    values = settle(last, masks, micro, received, first, second, scale, frame, pairs, pack)
    for k in range(early):
        out[k] = ready[2 * k][...]
    out[micro] = values[0]
    width = scale.shape[1]
    for which, cells in enumerate((inputs, act)):
        total = filter_grad(cells[micro], values[1 + which])
        for k in range(early):
            total = total + ready[2 * k + 1][which]
        for k in range(9):
            partial[which, k] = total[:, k * width : (k + 1) * width].astype(jnp.bfloat16)


def cross(cells, axis):
    count = lax.axis_size(axis)
    pairs = [(i, i + 1) for i in range(1, count - 1, 2)]
    return lax.ppermute(cells, axis, pairs + [(j, i) for i, j in pairs])


def swap(cells, axis):
    return lax.ppermute(cells, axis, [(i, i ^ 1) for i in range(lax.axis_size(axis))])


def in_place(apart, close, axis):
    even = (lax.axis_index(axis) & 1) == 0
    return (jnp.where(even, apart, close), jnp.where(even, close, apart))


def matrix_of(kernel):
    width = kernel.shape[-1]
    return jnp.transpose(jnp.flip(kernel, (0, 1)), (0, 3, 1, 2)).reshape(3 * width, 3 * width)


def sum_of_blocks(blocks, axes):
    parts = lax.all_to_all(blocks, axes, 0, 0, tiled=True)
    return jnp.sum(parts.astype(jnp.float32), axis=0)


def copies(block, axes):
    count = lax.axis_size(axes)
    return lax.all_to_all(jnp.broadcast_to(block[None], (count, *block.shape)), axes, 0, 0, tiled=True)


def write_kernel(core, half, *refs):
    out, lines, done = refs[-3:]
    stack, ring, rows, _ = half.shape
    chunk = stack * rows
    base = pl.multiple_of(core[0] * (ring * chunk), chunk)
    moves = []
    for x in range(ring):
        for z in range(stack):
            start = x * chunk + z * rows
            lines[start : start + rows] = half[z, x].astype(jnp.float32)
        source = lines.at[pl.ds(x * chunk, chunk)]
        move = pltpu.make_async_copy(source, out.at[pl.ds(base + x * chunk, chunk)], done.at[x])
        move.start()
        moves.append(move)
    for move in moves:
        move.wait()


def write_half(core, half, before):
    stack, ring, rows, width = half.shape
    lines = stack * ring * rows
    hbm = pl.BlockSpec(memory_space=pltpu.MemorySpace.HBM)
    return pl.pallas_call(
        write_kernel,
        in_specs=[SMEM, VMEM] + [hbm] * len(before),
        out_specs=hbm,
        out_shape=jax.ShapeDtypeStruct((2 * lines, width), jnp.float32),
        input_output_aliases={2: 0} if before else {},
        scratch_shapes=[pltpu.VMEM((lines, width), jnp.float32), pltpu.SemaphoreType.DMA((ring,))],
        compiler_params=PARAMS,
    )(core, half, *before)


def total_of(x, factor):
    near, stack, ring = (lax.axis_size(NEAR), lax.axis_size("row_0"), lax.axis_size("col_1"))
    width = x.shape[-1]
    part = sum_of_blocks(x.reshape(near, -1, width), NEAR).astype(jnp.bfloat16)
    part = part.reshape(stack, 1, -1, width)
    twice = jnp.broadcast_to(part, (stack, lax.axis_size("col_0"), *part.shape[2:]))
    own = sum_of_blocks(twice.reshape(-1, *part.shape[2:]), FAR)
    own = (own * factor).astype(jnp.bfloat16)
    half = copies(own[None], ("row_0", "col_1"))
    half = half.reshape(stack, ring, *own.shape)
    other = lax.ppermute(half, "row_1", [(0, 1), (1, 0)])
    core = lax.axis_index("row_1").astype(jnp.int32).reshape(1)
    written = write_half(core, half, [])
    return write_half(1 - core, other, [written])


def section_backward(section_input, first_pre, second_pre, out_grad, kernels, bn_scale, bn_shift):
    sections = lax.axis_size("section")
    last = (lax.axis_index("section") == sections - 1).astype(jnp.int32).reshape(1)
    even = ((lax.axis_index(COL) & 1) == 0).astype(jnp.int32).reshape(1)
    micros, rows_here, cols_here, width = out_grad.shape
    bf16 = jnp.bfloat16
    scale = bn_scale[0]
    two = (2, micros, rows_here)
    masks, inward, outward, act, scale = pl.pallas_call(
        prepare_kernel,
        name="prepare",
        in_specs=[SMEM] + [pl.BlockSpec(memory_space=pltpu.MemorySpace.HBM)] * 6,
        out_specs=[VMEM] * 5,
        out_shape=[
            jax.ShapeDtypeStruct((*two, cols_here, width), bf16),
            jax.ShapeDtypeStruct((*two, DEPTH, width), bf16),
            jax.ShapeDtypeStruct((*two, DEPTH, width), bf16),
            jax.ShapeDtypeStruct(out_grad.shape, bf16),
            jax.ShapeDtypeStruct(scale.shape, jnp.float32),
        ],
        scratch_shapes=[
            pltpu.VMEM((4, *out_grad.shape), bf16),
            pltpu.VMEM((2, *scale.shape), jnp.float32),
            pltpu.SemaphoreType.DMA((6,)),
        ],
        compiler_params=PARAMS,
    )(
        jnp.concatenate([last, even]),
        *[
            pltpu.with_memory_space_constraint(x, pltpu.MemorySpace.HBM)
            for x in (section_input[0], first_pre[0], second_pre[0], out_grad, scale, bn_shift[0])
        ],
    )
    left, right = in_place(cross(outward, COL), swap(inward, COL), COL)
    middle = cross(masks, ROW)
    sides = jnp.concatenate([left, right], axis=3)
    sides, kernels = lax.optimization_barrier((sides, kernels))
    band = jnp.concatenate([sides[:, :, :, :DEPTH], masks, sides[:, :, :, DEPTH:]], axis=3)
    corners = cross(sides, ROW)
    close = swap(band, ROW)
    first = matrix_of(kernels[0, 0])
    second = matrix_of(kernels[0, 1])
    apart = jnp.concatenate([corners[:, :, :, :DEPTH], middle, corners[:, :, :, DEPTH:]], axis=3)
    above, below = in_place(apart, close, ROW)
    masks = jnp.concatenate([above, band, below], axis=2)
    high, wide = masks.shape[2:4]
    pairs = [
        pltpu.VMEM((high // 2, 2, wide, width), jnp.float32),
        pltpu.VMEM((high // 2, 2 * (wide - 2 * PACKED), width), jnp.float32),
    ]

    received = [[]]
    for step in range(sections - 1):
        reach = 2 * (sections - 1 - step)
        rows = rows_here + 2 * reach
        shape = (rows, wide - 2 * NARROW, width)
        if step == 0:
            shape = (rows // 2, 2 * (wide - 2 * PACKED), width)
        active = (lax.axis_index("section") == sections - 1 - step).astype(jnp.int32).reshape(1)
        sent = []
        for micro in range(micros):
            taken = [received[-1][micro]] if step else []
            result = pl.pallas_call(
                functools.partial(stage_kernel, micro=micro, step=step, reach=reach),
                in_specs=[SMEM] + [VMEM] * (4 + len(taken)),
                out_specs=VMEM,
                out_shape=jax.ShapeDtypeStruct(shape, bf16),
                scratch_shapes=[pltpu.VMEM((high, wide, width), jnp.float32)] + pairs,
                compiler_params=PARAMS,
            )(active, masks, first, second, scale, *taken)
            pair = [(sections - 1 - step, sections - 2 - step)]
            sent.append(lax.ppermute(result, "section", pair))
        received.append(sent)
    scratch = [pltpu.VMEM((sections - 1, high, wide, width), jnp.float32)] + pairs
    common = (last, masks, first, second, scale)
    arrived = [[step[micro] for step in received[1:]] for micro in range(micros)]
    ready = []
    for micro in range(micros - 1):
        sums = jax.ShapeDtypeStruct((2, width, 9 * width), jnp.float32)
        ready += pl.pallas_call(
            functools.partial(early_kernel, micro=micro),
            in_specs=[SMEM] + [VMEM] * (6 + len(arrived[micro])),
            out_specs=[VMEM] * 2,
            out_shape=[jax.ShapeDtypeStruct(out_grad.shape[1:], bf16), sums],
            scratch_shapes=scratch,
            compiler_params=PARAMS,
        )(*common, section_input[0], act, *arrived[micro])
    taken = ready + arrived[-1]
    input_grad, partial = pl.pallas_call(
        functools.partial(last_kernel, micros=micros, early=micros - 1),
        name="last",
        in_specs=[SMEM] + [VMEM] * (6 + len(taken)),
        out_specs=[VMEM] * 2,
        out_shape=[
            jax.ShapeDtypeStruct(out_grad.shape, bf16),
            jax.ShapeDtypeStruct((2, 9, width, width), bf16),
        ],
        scratch_shapes=scratch,
        compiler_params=PARAMS,
    )(*common, section_input[0], act, *taken)
    pixels = micros * rows_here * lax.axis_size(ROW) * cols_here * lax.axis_size(COL)
    factor = 1.0 / jnp.sqrt(jnp.float32(pixels))
    total = total_of(partial, factor).reshape(2, 3, 3, width, width)
    return (input_grad[None], total[None])


def solution(mesh):
    split = Mesh(
        mesh.devices.reshape(mesh.shape["section"], 8, 2, 2, 4),
        ("section", "row_0", "row_1", "col_0", "col_1"),
    )
    in_specs = (
        P("section", None, ROW, COL, None),
        P("section", None, ROW, COL, None),
        P("section", None, ROW, COL, None),
        P(None, ROW, COL, None),
        P("section", None, None, None, None, None),
        P("section", None, None),
        P("section", None, None),
    )
    out_specs = (P("section", None, ROW, COL, None), P("section", None, None, None, None, None))
    return jax.shard_map(
        section_backward, mesh=split, in_specs=in_specs, out_specs=out_specs, check_vma=False
    )
```

profile of v0, /device:TPU:1, one launch (start us, length us, event | category | flops | bytes accessed | tf_op | source)
XLA Modules:
  0.0 109.4 jit_solution(11561010098513297172)
XLA Ops:
  0.7 0.1 pad_add_fusion.flags
  0.7 1.6 %prepare.1 = (bf16[2,2,8,16,128]{4,3,2,1,0:T(8,128)(2,1)S(1)}, bf16[2,2,8,8,128]{4,3,2,1,0:T(8,128)(2,1)S(1)}, bf16[2,2,8,8,128]{4,3,2,1,0:T(8,128)(2,1)S(1)}, b...) custom-call(s32[2]{0:T(128)S(1)} %pad_add_fusion.flags, bf16[2,8,16,128]{3,2,1,0:T(8,128)(2,1)} %bitcast.52, ...), custom_call_target="tpu_custom_call" | custom-call | tf_op jit(solution)/shard_map/prepare/pallas_call | solution.py:276
  2.4 0.7 collective-permute-start
  3.0 6.4 %collective-permute-start.1 = (bf16[2,2,8,8,128]{4,3,2,1,0:T(8,128)(2,1)S(1)}, bf16[2,2,8,8,128]{4,3,2,1,0:T(8,128)(2,1)S(1)}, u32[]{:S(2)}, u32[]{:S(2)}) collective-permute-start(bf16[2,2,8,8,128]{4,3,2,1,0:T(8,128)(2,1)S(1)} %get-tuple-element.14), channel_id=1, source_target_pairs={{0,1},{1,0},{2,3},{3,2},{4,5},{5,4},{6,7},{7,6},{8,9},{9,8},{10,11... | collective-permute-start | bytes 196616 | tf_op jit(solution)/shard_map/ppermute | solution.py:196
  9.4 5.1 %collective-permute-start.3 = (bf16[2,2,8,16,128]{4,3,2,1,0:T(8,128)(2,1)S(1)}, bf16[2,2,8,16,128]{4,3,2,1,0:T(8,128)(2,1)S(1)}, u32[]{:S(2)}, u32[]{:S(2)}) collective-permute-start(bf16[2,2,8,16,128]{4,3,2,1,0:T(8,128)(2,1)S(1)} %get-tuple-element.16), channel_id=1, source_target_pairs={{8,16},{24,32},{40,48},{56,64},{72,80},{88,96},{104,112},{16,8},{3... | collective-permute-start | bytes 393224 | tf_op jit(solution)/shard_map/ppermute | solution.py:192
  14.7 2.2 %collective-permute-start.2 = (bf16[2,2,8,16,128]{4,3,2,1,0:T(8,128)(2,1)S(1)}, bf16[2,2,8,16,128]{4,3,2,1,0:T(8,128)(2,1)S(1)}, u32[]{:S(2)}, u32[]{:S(2)}) collective-permute-start(bf16[2,2,8,16,128]{4,3,2,1,0:T(8,128)(2,1)S(1)} %pad_maximum_fusion.3), channel_id=1, source_target_pairs={{8,16},{24,32},{40,48},{56,64},{72,80},{88,96},{104,112},{16,8},{3... | collective-permute-start | bytes 393224 | tf_op jit(solution)/shard_map/ppermute | solution.py:192
  17.0 1.9 %collective-permute-start.4 = (bf16[2,2,8,32,128]{4,3,2,1,0:T(8,128)(2,1)S(1)}, bf16[2,2,8,32,128]{4,3,2,1,0:T(8,128)(2,1)S(1)}, u32[]{:S(2)}, u32[]{:S(2)}) collective-permute-start(bf16[2,2,8,32,128]{4,3,2,1,0:T(8,128)(2,1)S(1)} %pad_maximum_fusion.2), channel_id=1, source_target_pairs={{0,8},{8,0},{16,24},{24,16},{32,40},{40,32},{48,56},{56,48},{64,72... | collective-permute-start | bytes 786440 | tf_op jit(solution)/shard_map/ppermute | solution.py:196
  18.9 0.1 reverse_bitcast_fusion
  19.0 0.2 copy.23
  19.3 0.2 copy.22
  19.6 1.4 %collective-permute-done.2 = bf16[2,2,8,16,128]{4,3,2,1,0:T(8,128)(2,1)S(1)} collective-permute-done((bf16[2,2,8,16,128]{4,3,2,1,0:T(8,128)(2,1)S(1)}, bf16[2,2,8,16,128]{4,3,2,1,0:T(8,128)(2,1)S(1)}, u32[]{:S(2)}, u32[]{:S(2)}) %collective-permute-start.2) | collective-permute-done | bytes 131104 | tf_op jit(solution)/shard_map/ppermute | solution.py:192
  21.0 0.1 broadcast_select_fusion.1
  21.1 0.1 pad_maximum_fusion.refs_1_
  21.2 0.7 collective-permute-start.5
  21.9 0.7 collective-permute-start.8
  22.6 0.7 collective-permute-start.6
  23.3 0.7 collective-permute-start.9
  24.0 0.0 copy-start
  24.1 1.3 %collective-permute-start.7 = (bf16[12,24,128]{2,1,0:T(8,128)(2,1)S(1)}, bf16[12,24,128]{2,1,0:T(8,128)(2,1)S(1)}, u32[]{:S(2)}, u32[]{:S(2)}) collective-permute-start(bf16[12,24,128]{2,1,0:T(8,128)(2,1)S(1)} %shard_map.88), channel_id=1, source_target_pairs={{128,0},{129,1},{130,2},{131,3},{132,4},{133,5},{134,6},{135,7},{1... | collective-permute-start | bytes 221192 | tf_op jit(solution)/shard_map/ppermute | solution.py:339
  25.4 1.3 %collective-permute-start.10 = (bf16[12,24,128]{2,1,0:T(8,128)(2,1)S(1)}, bf16[12,24,128]{2,1,0:T(8,128)(2,1)S(1)}, u32[]{:S(2)}, u32[]{:S(2)}) collective-permute-start(bf16[12,24,128]{2,1,0:T(8,128)(2,1)S(1)} %shard_map.92), channel_id=1, source_target_pairs={{128,0},{129,1},{130,2},{131,3},{132,4},{133,5},{134,6},{135,7},{1... | collective-permute-start | bytes 221192 | tf_op jit(solution)/shard_map/ppermute | solution.py:339
  26.7 14.9 %collective-permute-done.7.refs_9_ = bf16[12,24,128]{2,1,0:T(8,128)(2,1)S(1)} collective-permute-done((bf16[12,24,128]{2,1,0:T(8,128)(2,1)S(1)}, bf16[12,24,128]{2,1,0:T(8,128)(2,1)S(1)}, u32[]{:S(2)}, u32[]{:S(2)}) %collective-permute-start.7) | collective-permute-done | bytes 73760 | tf_op jit(solution)/shard_map/ppermute | solution.py:339
  41.6 0.8 shard_map.89
  42.4 0.8 collective-permute-done.10.refs_11_
  43.2 1.3 %last.1 = (bf16[2,8,16,128]{3,2,1,0:T(8,128)(2,1)}, bf16[2,9,128,128]{3,2,1,0:T(8,128)(2,1)S(1)}) custom-call(s32[1]{0:T(128)} %bitcast.refs_0_, bf16[2,2,24,32,128]{4,3,2,1,0:T(8,128)(2,1)S(1)} %pad_maximum_fusion.refs_1_, bf16[384,384]{1,0:T(8,128)(2,1)S(1)} %bitcast.48, bf16[384,384]{1,0:T(8,128)(2,1)S(1)} %bitcast.40, ...), custom_call_target="tpu_custom_call" | custom-call | tf_op jit(solution)/shard_map/last/pallas_call | solution.py:356
  44.6 18.9 %all_to_all.15 = bf16[8,288,128]{2,1,0:T(8,128)(2,1)S(1)} all-to-all(bf16[8,288,128]{2,1,0:T(8,128)(2,1)S(1)} %bitcast.51), channel_id=1, replica_groups=mesh['section'=4,'row_0'=8,'row_1'=2,'col_0'=2,'col_1'=4] {'row_1','col_1'}, dimensions={0} | all-to-all | bytes 1179648 | tf_op jit(solution)/shard_map/all_to_all | solution.py:210
  63.5 0.1 reduce_sum.21
  63.7 23.2 %all_to_all.16 = bf16[16,36,128]{2,1,0:T(8,128)(2,1)S(1)} all-to-all(bf16[16,36,128]{2,1,0:T(8,128)(2,1)S(1)} %bitcast.58), channel_id=1, replica_groups=mesh['section'=4,'row_0'=8,'row_1'=2,'col_0'=2,'col_1'=4] {'row_0','col_0'}, dimensions={0} | all-to-all | bytes 294912 | tf_op jit(solution)/shard_map/all_to_all | solution.py:210
  87.0 14.1 %all_to_all.17 = bf16[32,1,36,128]{3,2,1,0:T(8,128)(2,1)S(1)} all-to-all(bf16[32,1,36,128]{3,2,1,0:T(8,128)(2,1)S(1)} %broadcast_in_dim.18), channel_id=1, replica_groups=mesh['section'=4,'row_0'=8,'row_1'=2,'col_0'=2,'col_1'=4] {'row_0','col_1'}, dimensions={0} | all-to-all | bytes 589824 | tf_op jit(solution)/shard_map/all_to_all | solution.py:216
  101.1 6.2 %collective-permute-start.11 = (bf16[8,4,36,128]{3,2,1,0:T(8,128)(2,1)S(1)}, bf16[8,4,36,128]{3,2,1,0:T(8,128)(2,1)S(1)}, u32[]{:S(2)}, u32[]{:S(2)}) collective-permute-start(bf16[8,4,36,128]{3,2,1,0:T(8,128)(2,1)S(1)} %bitcast.49), channel_id=1, source_target_pairs={{0,8},{8,0},{1,9},{9,1},{2,10},{10,2},{3,11},{11,3},{4,12},{12,4},... | collective-permute-start | bytes 884744 | tf_op jit(solution)/shard_map/ppermute | solution.py:262
  107.3 0.9 shard_map.93.refs_0_
  108.2 0.4 collective-permute-done.11.half
  108.5 0.9 shard_map.94
  (30 shorter events, 0.5 us)
Async XLA Ops:
  0.6 16.2 %copy-start.1 = (bf16[1,2,3,3,128,128]{5,4,3,2,1,0:T(8,128)(2,1)S(1)}, bf16[1,2,3,3,128,128]{5,4,3,2,1,0:T(8,128)(2,1)}, u32[]{:S(2)}) copy-start(bf16[1,2,3,3,128,128]{5,4,3,2,1,0:T(8,128)(2,1)} %param.11) | copy-start | bytes 1769476
  2.4 12.2 %collective-permute-start = (bf16[2,2,8,8,128]{4,3,2,1,0:T(8,128)(2,1)S(1)}, bf16[2,2,8,8,128]{4,3,2,1,0:T(8,128)(2,1)S(1)}, u32[]{:S(2)}, u32[]{:S(2)}) collective-permute-start(bf16[2,2,8,8,128]{4,3,2,1,0:T(8,128)(2,1)S(1)} %get-tuple-element.13), channel_id=1, source_target_pairs={{1,2},{3,4},{5,6},{2,1},{4,3},{6,5},{9,10},{11,12},{13,14},{10,9},... | collective-permute-start | bytes 196616 | tf_op jit(solution)/shard_map/ppermute | solution.py:192
  3.0 11.6 %collective-permute-start.1 = (bf16[2,2,8,8,128]{4,3,2,1,0:T(8,128)(2,1)S(1)}, bf16[2,2,8,8,128]{4,3,2,1,0:T(8,128)(2,1)S(1)}, u32[]{:S(2)}, u32[]{:S(2)}) collective-permute-start(bf16[2,2,8,8,128]{4,3,2,1,0:T(8,128)(2,1)S(1)} %get-tuple-element.14), channel_id=1, source_target_pairs={{0,1},{1,0},{2,3},{3,2},{4,5},{5,4},{6,7},{7,6},{8,9},{9,8},{10,11... | collective-permute-start | bytes 196616 | tf_op jit(solution)/shard_map/ppermute | solution.py:196
  9.4 11.6 %collective-permute-start.3 = (bf16[2,2,8,16,128]{4,3,2,1,0:T(8,128)(2,1)S(1)}, bf16[2,2,8,16,128]{4,3,2,1,0:T(8,128)(2,1)S(1)}, u32[]{:S(2)}, u32[]{:S(2)}) collective-permute-start(bf16[2,2,8,16,128]{4,3,2,1,0:T(8,128)(2,1)S(1)} %get-tuple-element.16), channel_id=1, source_target_pairs={{8,16},{24,32},{40,48},{56,64},{72,80},{88,96},{104,112},{16,8},{3... | collective-permute-start | bytes 393224 | tf_op jit(solution)/shard_map/ppermute | solution.py:192
  14.7 6.3 %collective-permute-start.2 = (bf16[2,2,8,16,128]{4,3,2,1,0:T(8,128)(2,1)S(1)}, bf16[2,2,8,16,128]{4,3,2,1,0:T(8,128)(2,1)S(1)}, u32[]{:S(2)}, u32[]{:S(2)}) collective-permute-start(bf16[2,2,8,16,128]{4,3,2,1,0:T(8,128)(2,1)S(1)} %pad_maximum_fusion.3), channel_id=1, source_target_pairs={{8,16},{24,32},{40,48},{56,64},{72,80},{88,96},{104,112},{16,8},{3... | collective-permute-start | bytes 393224 | tf_op jit(solution)/shard_map/ppermute | solution.py:192
  17.0 4.0 %collective-permute-start.4 = (bf16[2,2,8,32,128]{4,3,2,1,0:T(8,128)(2,1)S(1)}, bf16[2,2,8,32,128]{4,3,2,1,0:T(8,128)(2,1)S(1)}, u32[]{:S(2)}, u32[]{:S(2)}) collective-permute-start(bf16[2,2,8,32,128]{4,3,2,1,0:T(8,128)(2,1)S(1)} %pad_maximum_fusion.2), channel_id=1, source_target_pairs={{0,8},{8,0},{16,24},{24,16},{32,40},{40,32},{48,56},{56,48},{64,72... | collective-permute-start | bytes 786440 | tf_op jit(solution)/shard_map/ppermute | solution.py:196
  21.2 1.4 %collective-permute-start.5 = (bf16[10,56,128]{2,1,0:T(8,128)(2,1)S(1)}, bf16[10,56,128]{2,1,0:T(8,128)(2,1)S(1)}, u32[]{:S(2)}, u32[]{:S(2)}) collective-permute-start(bf16[10,56,128]{2,1,0:T(8,128)(2,1)S(1)} %shard_map.86), channel_id=1, source_target_pairs={{384,256},{385,257},{386,258},{387,259},{388,260},{389,261},{390,2... | collective-permute-start | bytes 430088 | tf_op jit(solution)/shard_map/ppermute | solution.py:339
  21.9 1.4 %collective-permute-start.8 = (bf16[10,56,128]{2,1,0:T(8,128)(2,1)S(1)}, bf16[10,56,128]{2,1,0:T(8,128)(2,1)S(1)}, u32[]{:S(2)}, u32[]{:S(2)}) collective-permute-start(bf16[10,56,128]{2,1,0:T(8,128)(2,1)S(1)} %shard_map.90), channel_id=1, source_target_pairs={{384,256},{385,257},{386,258},{387,259},{388,260},{389,261},{390,2... | collective-permute-start | bytes 430088 | tf_op jit(solution)/shard_map/ppermute | solution.py:339
  22.6 1.4 %collective-permute-start.6 = (bf16[16,24,128]{2,1,0:T(8,128)(2,1)S(1)}, bf16[16,24,128]{2,1,0:T(8,128)(2,1)S(1)}, u32[]{:S(2)}, u32[]{:S(2)}) collective-permute-start(bf16[16,24,128]{2,1,0:T(8,128)(2,1)S(1)} %shard_map.87), channel_id=1, source_target_pairs={{256,128},{257,129},{258,130},{259,131},{260,132},{261,133},{262,1... | collective-permute-start | bytes 294920 | tf_op jit(solution)/shard_map/ppermute | solution.py:339
  23.3 2.0 %collective-permute-start.9 = (bf16[16,24,128]{2,1,0:T(8,128)(2,1)S(1)}, bf16[16,24,128]{2,1,0:T(8,128)(2,1)S(1)}, u32[]{:S(2)}, u32[]{:S(2)}) collective-permute-start(bf16[16,24,128]{2,1,0:T(8,128)(2,1)S(1)} %shard_map.91), channel_id=1, source_target_pairs={{256,128},{257,129},{258,130},{259,131},{260,132},{261,133},{262,1... | collective-permute-start | bytes 294920 | tf_op jit(solution)/shard_map/ppermute | solution.py:339
  24.0 17.6 %copy-start = (bf16[1,2,8,16,128]{4,3,2,1,0:T(8,128)(2,1)S(1)}, bf16[1,2,8,16,128]{4,3,2,1,0:T(8,128)(2,1)}, u32[]{:S(2)}) copy-start(bf16[1,2,8,16,128]{4,3,2,1,0:T(8,128)(2,1)} %param.7) | copy-start | bytes 196612
  24.1 17.6 %collective-permute-start.7 = (bf16[12,24,128]{2,1,0:T(8,128)(2,1)S(1)}, bf16[12,24,128]{2,1,0:T(8,128)(2,1)S(1)}, u32[]{:S(2)}, u32[]{:S(2)}) collective-permute-start(bf16[12,24,128]{2,1,0:T(8,128)(2,1)S(1)} %shard_map.88), channel_id=1, source_target_pairs={{128,0},{129,1},{130,2},{131,3},{132,4},{133,5},{134,6},{135,7},{1... | collective-permute-start | bytes 221192 | tf_op jit(solution)/shard_map/ppermute | solution.py:339
  25.4 17.9 %collective-permute-start.10 = (bf16[12,24,128]{2,1,0:T(8,128)(2,1)S(1)}, bf16[12,24,128]{2,1,0:T(8,128)(2,1)S(1)}, u32[]{:S(2)}, u32[]{:S(2)}) collective-permute-start(bf16[12,24,128]{2,1,0:T(8,128)(2,1)S(1)} %shard_map.92), channel_id=1, source_target_pairs={{128,0},{129,1},{130,2},{131,3},{132,4},{133,5},{134,6},{135,7},{1... | collective-permute-start | bytes 221192 | tf_op jit(solution)/shard_map/ppermute | solution.py:339
  101.1 7.4 %collective-permute-start.11 = (bf16[8,4,36,128]{3,2,1,0:T(8,128)(2,1)S(1)}, bf16[8,4,36,128]{3,2,1,0:T(8,128)(2,1)S(1)}, u32[]{:S(2)}, u32[]{:S(2)}) collective-permute-start(bf16[8,4,36,128]{3,2,1,0:T(8,128)(2,1)S(1)} %bitcast.49), channel_id=1, source_target_pairs={{0,8},{8,0},{1,9},{9,1},{2,10},{10,2},{3,11},{11,3},{4,12},{12,4},... | collective-permute-start | bytes 884744 | tf_op jit(solution)/shard_map/ppermute | solution.py:262
where the time goes:
time: 110 us; the launch traced here: 109 us
  blocking collectives  56.2 us (51%)
  starting transfers between devices  27.7 us (25%)
  waiting for transfers between devices  17.5 us (16%)
  Pallas kernels  5.52 us (5%)
    all_to_all x2, blocking collectives, sum_of_blocks(): parts = lax.all_to_all(blocks, axes, 0, 0, tiled=True)  42.2 us
    ppermute x6, waiting for transfers between devices, section_backward(): sent.append(lax.ppermute(result, 'section', pair))  15.8 us
    all_to_all x1, blocking collectives, copies(): lax.all_to_all(jnp.broadcast_to(block[None], (count, *block.shape)), axes...  14.1 us
    ppermute x2, starting transfers between devices, swap(): lax.ppermute(cells, axis, [(i, i ^ 1) for i in range(lax.axis_size(axis))])  8.31 us
    ppermute x3, starting transfers between devices, cross(): return lax.ppermute(cells, axis, pairs + [(j, i) for i, j in pairs])  7.97 us
    ppermute x1, starting transfers between devices, total_of(): other = lax.ppermute(half, 'row_1', [(0, 1), (1, 0)])  6.18 us
    ppermute x6, starting transfers between devices, section_backward(): sent.append(lax.ppermute(result, 'section', pair))  5.26 us
  transfers between devices with their start and end apart: 12, of which 4 were waited for; matrix products, arithmetic and copies ran while one was open for 1% of the time, Pallas kernels for 2%

commit v1 on v0

--- a/solution.py
+++ b/solution.py
@@ -82,7 +82,7 @@
     pairs[:half] = cells.reshape(half, 2, cols, width)
     for k in range(2):
         pack[:half, k * kept : (k + 1) * kept] = pairs[:half, k, cut : cut + kept]
-    return pack[:half]
+    return pack[:half, : 2 * kept]
 
 
 def unpacked(cells, pairs, pack, skip):
@@ -90,7 +90,7 @@
     kept = cells.shape[1] // 2
     cols = pairs.shape[2]
     cut = (cols - kept) // 2
-    pack[:half] = cells[skip // 2 : skip // 2 + half].astype(jnp.float32)
+    pack[:half, : 2 * kept] = cells[skip // 2 : skip // 2 + half].astype(jnp.float32)
     pairs[:half] = jnp.zeros((half, *pairs.shape[1:]), jnp.float32)
     for k in range(2):
         pairs[:half, k, cut : cut + kept] = pack[:half, k * kept : (k + 1) * kept]
@@ -116,11 +116,11 @@
         elif step > 1:
             incoming = widened(received[0], frame, 0)
         result, _, _ = unit(masks, micro, incoming, first, second, scale, reach)
-        if step:
+        if step == 1:
             frame[: result.shape[0]] = result
             result = frame[: result.shape[0], NARROW : result.shape[1] - NARROW]
         else:
-            result = packed(result, pairs, pack, PACKED)
+            result = packed(result, pairs, pack, PACKED if step == 0 else DEPTH - reach)
         out[...] = result.astype(jnp.bfloat16)
 
 
@@ -148,7 +148,7 @@
     steps = len(received)
     for step, cells in enumerate(received):
         skip = 2 * (steps - 1 - step)
-        if step:
+        if step == 1:
             incoming = incoming + widened(cells, frame.at[step], skip)
         else:
             incoming = incoming + unpacked(cells, pairs, pack, skip)
@@ -323,6 +323,8 @@
         shape = (rows, wide - 2 * NARROW, width)
         if step == 0:
             shape = (rows // 2, 2 * (wide - 2 * PACKED), width)
+        elif step == 2:
+            shape = (rows // 2, 2 * (wide - 2 * (DEPTH - reach)), width)
         active = (lax.axis_index("section") == sections - 1 - step).astype(jnp.int32).reshape(1)
         sent = []
         for micro in range(micros):

time: 110 us -> 110 us (level)
  no operation moved by 1% of the time
where the time goes in v1:
time: 110 us; the launch traced here: 109 us
  blocking collectives  56.2 us (51%)
  starting transfers between devices  27.7 us (25%)
  waiting for transfers between devices  17.4 us (16%)
  Pallas kernels  5.51 us (5%)
    all_to_all x2, blocking collectives, sum_of_blocks(): parts = lax.all_to_all(blocks, axes, 0, 0, tiled=True)  42.2 us
    ppermute x6, waiting for transfers between devices, section_backward(): sent.append(lax.ppermute(result, 'section', pair))  15.7 us
    all_to_all x1, blocking collectives, copies(): lax.all_to_all(jnp.broadcast_to(block[None], (count, *block.shape)), axes...  14.1 us
    ppermute x2, starting transfers between devices, swap(): lax.ppermute(cells, axis, [(i, i ^ 1) for i in range(lax.axis_size(axis))])  8.31 us
    ppermute x3, starting transfers between devices, cross(): return lax.ppermute(cells, axis, pairs + [(j, i) for i, j in pairs])  7.97 us
    ppermute x1, starting transfers between devices, total_of(): other = lax.ppermute(half, 'row_1', [(0, 1), (1, 0)])  6.18 us
    ppermute x6, starting transfers between devices, section_backward(): sent.append(lax.ppermute(result, 'section', pair))  5.26 us
  transfers between devices with their start and end apart: 12, of which 4 were waited for; matrix products, arithmetic and copies ran while one was open for 1% of the time, Pallas kernels for 2%

profile of v1, /device:TPU:1, one launch (start us, length us, event | category | flops | bytes accessed | tf_op | source)
XLA Modules:
  0.0 109.2 jit_solution(4005620844792773509)
XLA Ops:
  0.7 0.1 pad_add_fusion.flags
  0.7 1.6 %prepare.1 = (bf16[2,2,8,16,128]{4,3,2,1,0:T(8,128)(2,1)S(1)}, bf16[2,2,8,8,128]{4,3,2,1,0:T(8,128)(2,1)S(1)}, bf16[2,2,8,8,128]{4,3,2,1,0:T(8,128)(2,1)S(1)}, b...) custom-call(s32[2]{0:T(128)S(1)} %pad_add_fusion.flags, bf16[2,8,16,128]{3,2,1,0:T(8,128)(2,1)} %bitcast.51, ...), custom_call_target="tpu_custom_call" | custom-call | tf_op jit(solution)/shard_map/prepare/pallas_call | solution.py:276
  2.4 0.7 collective-permute-start
  3.0 6.4 %collective-permute-start.1 = (bf16[2,2,8,8,128]{4,3,2,1,0:T(8,128)(2,1)S(1)}, bf16[2,2,8,8,128]{4,3,2,1,0:T(8,128)(2,1)S(1)}, u32[]{:S(2)}, u32[]{:S(2)}) collective-permute-start(bf16[2,2,8,8,128]{4,3,2,1,0:T(8,128)(2,1)S(1)} %get-tuple-element.14), channel_id=1, source_target_pairs={{0,1},{1,0},{2,3},{3,2},{4,5},{5,4},{6,7},{7,6},{8,9},{9,8},{10,11... | collective-permute-start | bytes 196616 | tf_op jit(solution)/shard_map/ppermute | solution.py:196
  9.4 5.1 %collective-permute-start.3 = (bf16[2,2,8,16,128]{4,3,2,1,0:T(8,128)(2,1)S(1)}, bf16[2,2,8,16,128]{4,3,2,1,0:T(8,128)(2,1)S(1)}, u32[]{:S(2)}, u32[]{:S(2)}) collective-permute-start(bf16[2,2,8,16,128]{4,3,2,1,0:T(8,128)(2,1)S(1)} %get-tuple-element.16), channel_id=1, source_target_pairs={{8,16},{24,32},{40,48},{56,64},{72,80},{88,96},{104,112},{16,8},{3... | collective-permute-start | bytes 393224 | tf_op jit(solution)/shard_map/ppermute | solution.py:192
  14.7 2.2 %collective-permute-start.2 = (bf16[2,2,8,16,128]{4,3,2,1,0:T(8,128)(2,1)S(1)}, bf16[2,2,8,16,128]{4,3,2,1,0:T(8,128)(2,1)S(1)}, u32[]{:S(2)}, u32[]{:S(2)}) collective-permute-start(bf16[2,2,8,16,128]{4,3,2,1,0:T(8,128)(2,1)S(1)} %pad_maximum_fusion.3), channel_id=1, source_target_pairs={{8,16},{24,32},{40,48},{56,64},{72,80},{88,96},{104,112},{16,8},{3... | collective-permute-start | bytes 393224 | tf_op jit(solution)/shard_map/ppermute | solution.py:192
  17.0 1.9 %collective-permute-start.4 = (bf16[2,2,8,32,128]{4,3,2,1,0:T(8,128)(2,1)S(1)}, bf16[2,2,8,32,128]{4,3,2,1,0:T(8,128)(2,1)S(1)}, u32[]{:S(2)}, u32[]{:S(2)}) collective-permute-start(bf16[2,2,8,32,128]{4,3,2,1,0:T(8,128)(2,1)S(1)} %pad_maximum_fusion.2), channel_id=1, source_target_pairs={{0,8},{8,0},{16,24},{24,16},{32,40},{40,32},{48,56},{56,48},{64,72... | collective-permute-start | bytes 786440 | tf_op jit(solution)/shard_map/ppermute | solution.py:196
  18.9 0.1 reverse_bitcast_fusion
  19.0 0.2 copy.23
  19.3 0.2 copy.22
  19.6 1.4 %collective-permute-done.2 = bf16[2,2,8,16,128]{4,3,2,1,0:T(8,128)(2,1)S(1)} collective-permute-done((bf16[2,2,8,16,128]{4,3,2,1,0:T(8,128)(2,1)S(1)}, bf16[2,2,8,16,128]{4,3,2,1,0:T(8,128)(2,1)S(1)}, u32[]{:S(2)}, u32[]{:S(2)}) %collective-permute-start.2) | collective-permute-done | bytes 131104 | tf_op jit(solution)/shard_map/ppermute | solution.py:192
  21.0 0.1 broadcast_select_fusion.1
  21.1 0.1 pad_maximum_fusion.refs_1_
  21.2 0.7 collective-permute-start.5
  21.9 0.7 collective-permute-start.8
  22.6 0.7 collective-permute-start.6
  23.3 0.7 collective-permute-start.9
  24.0 0.0 copy-start
  24.1 1.3 %collective-permute-start.7 = (bf16[6,40,128]{2,1,0:T(8,128)(2,1)S(1)}, bf16[6,40,128]{2,1,0:T(8,128)(2,1)S(1)}, u32[]{:S(2)}, u32[]{:S(2)}) collective-permute-start(bf16[6,40,128]{2,1,0:T(8,128)(2,1)S(1)} %shard_map.88), channel_id=1, source_target_pairs={{128,0},{129,1},{130,2},{131,3},{132,4},{133,5},{134,6},{135,7},{1... | collective-permute-start | bytes 184328 | tf_op jit(solution)/shard_map/ppermute | solution.py:341
  25.4 1.3 %collective-permute-start.10 = (bf16[6,40,128]{2,1,0:T(8,128)(2,1)S(1)}, bf16[6,40,128]{2,1,0:T(8,128)(2,1)S(1)}, u32[]{:S(2)}, u32[]{:S(2)}) collective-permute-start(bf16[6,40,128]{2,1,0:T(8,128)(2,1)S(1)} %shard_map.92), channel_id=1, source_target_pairs={{128,0},{129,1},{130,2},{131,3},{132,4},{133,5},{134,6},{135,7},{1... | collective-permute-start | bytes 184328 | tf_op jit(solution)/shard_map/ppermute | solution.py:341
  26.7 14.7 %collective-permute-done.7.refs_9_ = bf16[6,40,128]{2,1,0:T(8,128)(2,1)S(1)} collective-permute-done((bf16[6,40,128]{2,1,0:T(8,128)(2,1)S(1)}, bf16[6,40,128]{2,1,0:T(8,128)(2,1)S(1)}, u32[]{:S(2)}, u32[]{:S(2)}) %collective-permute-start.7) | collective-permute-done | bytes 61472 | tf_op jit(solution)/shard_map/ppermute | solution.py:341
  41.4 0.8 shard_map.89
  42.2 1.0 collective-permute-done.10.refs_11_
  43.1 1.3 %last.1 = (bf16[2,8,16,128]{3,2,1,0:T(8,128)(2,1)}, bf16[2,9,128,128]{3,2,1,0:T(8,128)(2,1)S(1)}) custom-call(s32[1]{0:T(128)} %bitcast.refs_0_, bf16[2,2,24,32,128]{4,3,2,1,0:T(8,128)(2,1)S(1)} %pad_maximum_fusion.refs_1_, bf16[384,384]{1,0:T(8,128)(2,1)S(1)} %bitcast.48, bf16[384,384]{1,0:T(8,128)(2,1)S(1)} %bitcast.40, ...), custom_call_target="tpu_custom_call" | custom-call | tf_op jit(solution)/shard_map/last/pallas_call | solution.py:358
  44.5 18.9 %all_to_all.15 = bf16[8,288,128]{2,1,0:T(8,128)(2,1)S(1)} all-to-all(bf16[8,288,128]{2,1,0:T(8,128)(2,1)S(1)} %bitcast.54), channel_id=1, replica_groups=mesh['section'=4,'row_0'=8,'row_1'=2,'col_0'=2,'col_1'=4] {'row_1','col_1'}, dimensions={0} | all-to-all | bytes 1179648 | tf_op jit(solution)/shard_map/all_to_all | solution.py:210
  63.4 0.1 reduce_sum.21
  63.6 23.2 %all_to_all.16 = bf16[16,36,128]{2,1,0:T(8,128)(2,1)S(1)} all-to-all(bf16[16,36,128]{2,1,0:T(8,128)(2,1)S(1)} %bitcast.58), channel_id=1, replica_groups=mesh['section'=4,'row_0'=8,'row_1'=2,'col_0'=2,'col_1'=4] {'row_0','col_0'}, dimensions={0} | all-to-all | bytes 294912 | tf_op jit(solution)/shard_map/all_to_all | solution.py:210
  86.9 14.1 %all_to_all.17 = bf16[32,1,36,128]{3,2,1,0:T(8,128)(2,1)S(1)} all-to-all(bf16[32,1,36,128]{3,2,1,0:T(8,128)(2,1)S(1)} %broadcast_in_dim.18), channel_id=1, replica_groups=mesh['section'=4,'row_0'=8,'row_1'=2,'col_0'=2,'col_1'=4] {'row_0','col_1'}, dimensions={0} | all-to-all | bytes 589824 | tf_op jit(solution)/shard_map/all_to_all | solution.py:216
  101.0 6.2 %collective-permute-start.11 = (bf16[8,4,36,128]{3,2,1,0:T(8,128)(2,1)S(1)}, bf16[8,4,36,128]{3,2,1,0:T(8,128)(2,1)S(1)}, u32[]{:S(2)}, u32[]{:S(2)}) collective-permute-start(bf16[8,4,36,128]{3,2,1,0:T(8,128)(2,1)S(1)} %bitcast.49), channel_id=1, source_target_pairs={{0,8},{8,0},{1,9},{9,1},{2,10},{10,2},{3,11},{11,3},{4,12},{12,4},... | collective-permute-start | bytes 884744 | tf_op jit(solution)/shard_map/ppermute | solution.py:262
  107.2 0.9 shard_map.93.refs_0_
  108.0 0.4 collective-permute-done.11.half
  108.4 0.9 shard_map.94
  (30 shorter events, 0.5 us)
Async XLA Ops:
  0.6 16.2 %copy-start.1 = (bf16[1,2,3,3,128,128]{5,4,3,2,1,0:T(8,128)(2,1)S(1)}, bf16[1,2,3,3,128,128]{5,4,3,2,1,0:T(8,128)(2,1)}, u32[]{:S(2)}) copy-start(bf16[1,2,3,3,128,128]{5,4,3,2,1,0:T(8,128)(2,1)} %param.11) | copy-start | bytes 1769476
  2.4 12.2 %collective-permute-start = (bf16[2,2,8,8,128]{4,3,2,1,0:T(8,128)(2,1)S(1)}, bf16[2,2,8,8,128]{4,3,2,1,0:T(8,128)(2,1)S(1)}, u32[]{:S(2)}, u32[]{:S(2)}) collective-permute-start(bf16[2,2,8,8,128]{4,3,2,1,0:T(8,128)(2,1)S(1)} %get-tuple-element.13), channel_id=1, source_target_pairs={{1,2},{3,4},{5,6},{2,1},{4,3},{6,5},{9,10},{11,12},{13,14},{10,9},... | collective-permute-start | bytes 196616 | tf_op jit(solution)/shard_map/ppermute | solution.py:192
  3.0 11.6 %collective-permute-start.1 = (bf16[2,2,8,8,128]{4,3,2,1,0:T(8,128)(2,1)S(1)}, bf16[2,2,8,8,128]{4,3,2,1,0:T(8,128)(2,1)S(1)}, u32[]{:S(2)}, u32[]{:S(2)}) collective-permute-start(bf16[2,2,8,8,128]{4,3,2,1,0:T(8,128)(2,1)S(1)} %get-tuple-element.14), channel_id=1, source_target_pairs={{0,1},{1,0},{2,3},{3,2},{4,5},{5,4},{6,7},{7,6},{8,9},{9,8},{10,11... | collective-permute-start | bytes 196616 | tf_op jit(solution)/shard_map/ppermute | solution.py:196
  9.4 11.6 %collective-permute-start.3 = (bf16[2,2,8,16,128]{4,3,2,1,0:T(8,128)(2,1)S(1)}, bf16[2,2,8,16,128]{4,3,2,1,0:T(8,128)(2,1)S(1)}, u32[]{:S(2)}, u32[]{:S(2)}) collective-permute-start(bf16[2,2,8,16,128]{4,3,2,1,0:T(8,128)(2,1)S(1)} %get-tuple-element.16), channel_id=1, source_target_pairs={{8,16},{24,32},{40,48},{56,64},{72,80},{88,96},{104,112},{16,8},{3... | collective-permute-start | bytes 393224 | tf_op jit(solution)/shard_map/ppermute | solution.py:192
  14.7 6.3 %collective-permute-start.2 = (bf16[2,2,8,16,128]{4,3,2,1,0:T(8,128)(2,1)S(1)}, bf16[2,2,8,16,128]{4,3,2,1,0:T(8,128)(2,1)S(1)}, u32[]{:S(2)}, u32[]{:S(2)}) collective-permute-start(bf16[2,2,8,16,128]{4,3,2,1,0:T(8,128)(2,1)S(1)} %pad_maximum_fusion.3), channel_id=1, source_target_pairs={{8,16},{24,32},{40,48},{56,64},{72,80},{88,96},{104,112},{16,8},{3... | collective-permute-start | bytes 393224 | tf_op jit(solution)/shard_map/ppermute | solution.py:192
  17.0 4.0 %collective-permute-start.4 = (bf16[2,2,8,32,128]{4,3,2,1,0:T(8,128)(2,1)S(1)}, bf16[2,2,8,32,128]{4,3,2,1,0:T(8,128)(2,1)S(1)}, u32[]{:S(2)}, u32[]{:S(2)}) collective-permute-start(bf16[2,2,8,32,128]{4,3,2,1,0:T(8,128)(2,1)S(1)} %pad_maximum_fusion.2), channel_id=1, source_target_pairs={{0,8},{8,0},{16,24},{24,16},{32,40},{40,32},{48,56},{56,48},{64,72... | collective-permute-start | bytes 786440 | tf_op jit(solution)/shard_map/ppermute | solution.py:196
  21.2 1.4 %collective-permute-start.5 = (bf16[10,56,128]{2,1,0:T(8,128)(2,1)S(1)}, bf16[10,56,128]{2,1,0:T(8,128)(2,1)S(1)}, u32[]{:S(2)}, u32[]{:S(2)}) collective-permute-start(bf16[10,56,128]{2,1,0:T(8,128)(2,1)S(1)} %shard_map.86), channel_id=1, source_target_pairs={{384,256},{385,257},{386,258},{387,259},{388,260},{389,261},{390,2... | collective-permute-start | bytes 430088 | tf_op jit(solution)/shard_map/ppermute | solution.py:341
  21.9 1.4 %collective-permute-start.8 = (bf16[10,56,128]{2,1,0:T(8,128)(2,1)S(1)}, bf16[10,56,128]{2,1,0:T(8,128)(2,1)S(1)}, u32[]{:S(2)}, u32[]{:S(2)}) collective-permute-start(bf16[10,56,128]{2,1,0:T(8,128)(2,1)S(1)} %shard_map.90), channel_id=1, source_target_pairs={{384,256},{385,257},{386,258},{387,259},{388,260},{389,261},{390,2... | collective-permute-start | bytes 430088 | tf_op jit(solution)/shard_map/ppermute | solution.py:341
  22.6 1.4 %collective-permute-start.6 = (bf16[16,24,128]{2,1,0:T(8,128)(2,1)S(1)}, bf16[16,24,128]{2,1,0:T(8,128)(2,1)S(1)}, u32[]{:S(2)}, u32[]{:S(2)}) collective-permute-start(bf16[16,24,128]{2,1,0:T(8,128)(2,1)S(1)} %shard_map.87), channel_id=1, source_target_pairs={{256,128},{257,129},{258,130},{259,131},{260,132},{261,133},{262,1... | collective-permute-start | bytes 294920 | tf_op jit(solution)/shard_map/ppermute | solution.py:341
  23.3 2.0 %collective-permute-start.9 = (bf16[16,24,128]{2,1,0:T(8,128)(2,1)S(1)}, bf16[16,24,128]{2,1,0:T(8,128)(2,1)S(1)}, u32[]{:S(2)}, u32[]{:S(2)}) collective-permute-start(bf16[16,24,128]{2,1,0:T(8,128)(2,1)S(1)} %shard_map.91), channel_id=1, source_target_pairs={{256,128},{257,129},{258,130},{259,131},{260,132},{261,133},{262,1... | collective-permute-start | bytes 294920 | tf_op jit(solution)/shard_map/ppermute | solution.py:341
  24.0 17.4 %copy-start = (bf16[1,2,8,16,128]{4,3,2,1,0:T(8,128)(2,1)S(1)}, bf16[1,2,8,16,128]{4,3,2,1,0:T(8,128)(2,1)}, u32[]{:S(2)}) copy-start(bf16[1,2,8,16,128]{4,3,2,1,0:T(8,128)(2,1)} %param.7) | copy-start | bytes 196612
  24.1 17.3 %collective-permute-start.7 = (bf16[6,40,128]{2,1,0:T(8,128)(2,1)S(1)}, bf16[6,40,128]{2,1,0:T(8,128)(2,1)S(1)}, u32[]{:S(2)}, u32[]{:S(2)}) collective-permute-start(bf16[6,40,128]{2,1,0:T(8,128)(2,1)S(1)} %shard_map.88), channel_id=1, source_target_pairs={{128,0},{129,1},{130,2},{131,3},{132,4},{133,5},{134,6},{135,7},{1... | collective-permute-start | bytes 184328 | tf_op jit(solution)/shard_map/ppermute | solution.py:341
  25.4 17.7 %collective-permute-start.10 = (bf16[6,40,128]{2,1,0:T(8,128)(2,1)S(1)}, bf16[6,40,128]{2,1,0:T(8,128)(2,1)S(1)}, u32[]{:S(2)}, u32[]{:S(2)}) collective-permute-start(bf16[6,40,128]{2,1,0:T(8,128)(2,1)S(1)} %shard_map.92), channel_id=1, source_target_pairs={{128,0},{129,1},{130,2},{131,3},{132,4},{133,5},{134,6},{135,7},{1... | collective-permute-start | bytes 184328 | tf_op jit(solution)/shard_map/ppermute | solution.py:341
  101.0 7.4 %collective-permute-start.11 = (bf16[8,4,36,128]{3,2,1,0:T(8,128)(2,1)S(1)}, bf16[8,4,36,128]{3,2,1,0:T(8,128)(2,1)S(1)}, u32[]{:S(2)}, u32[]{:S(2)}) collective-permute-start(bf16[8,4,36,128]{3,2,1,0:T(8,128)(2,1)S(1)} %bitcast.49), channel_id=1, source_target_pairs={{0,8},{8,0},{1,9},{9,1},{2,10},{10,2},{3,11},{11,3},{4,12},{12,4},... | collective-permute-start | bytes 884744 | tf_op jit(solution)/shard_map/ppermute | solution.py:262
